TPU v7x, 32 devices: a whole 2x2x4 slice. The times are simulated.
32 devices in a mesh: row: 4 (over z), col: 8 (over y, x, core).
Axes of the slice: x: 2, y: 2, z: 4, core: 2. Of those that a mesh axis runs over, the one named last changes fastest.
Arguments:
- block_values: float32 [65536, 128], P(('row', 'col')), may hold values from -6 to 6
- block_owner: int32 [65536, 1], P(('row', 'col')), may hold values from 0 to 31; in each aligned block of 2048 rows (0 to 2047, 2048 to 4095, ...) at most 128 rows name the same one
- block_offset: int32 [65536], P(('row', 'col')), may hold values from 0 to 39
- block_tiles: int32 [65536], P(('row', 'col')), may hold values from 0 to 107
Outputs:
- summed: float32 [1280, 13824], P(('row', 'col'))
- occupancy: int32 [10, 108], replicated
Inputs may be any that keep to these rules, and one draw needn't show every extreme that they name: `block_owner`: among the rows of one device no owner is named more than 128 times, a bound that some block reaches.
All inputs are finite; a program needn't handle non-finite values.
Results may differ from a plain program's by a relative error of at most 0.0003.
Values sent between devices are 32-bit elements; how exact they have to be, the bound alone decides.
A program may use at most 64 MiB of HBM per device.

v0:
```python
import math

import jax
import jax.numpy as jnp
from jax import lax
from jax.sharding import PartitionSpec as P

F = 13824
TILE = 128
ROWS_DEV = 40


def body(block_values, block_owner, block_offset, block_tiles):
    tiles_count = F // TILE
    size_row = lax.axis_size("row")
    size_col = lax.axis_size("col")
    devices_all = size_row * size_col
    local_blocks = block_values.shape[0]
    capacity = 2 * local_blocks // devices_all
    slots_total = devices_all * capacity
    owner = block_owner[:, 0]
    sentinel = ROWS_DEV * tiles_count
    owner_hot = (owner[:, None] == jnp.arange(devices_all, dtype=jnp.int32)[None, :]).astype(
        jnp.bfloat16
    )
    positions = jnp.arange(local_blocks, dtype=jnp.int32)
    earlier = (positions[None, :] < positions[:, None]).astype(jnp.bfloat16)
    before = jnp.dot(earlier, owner_hot, preferred_element_type=jnp.float32)
    slot = jnp.sum(before * owner_hot.astype(jnp.float32), axis=1).astype(jnp.int32)
    target = owner * capacity + slot
    local_keys = (block_offset * tiles_count + block_tiles).astype(jnp.float32)
    slot_step = math.gcd(slots_total, 512)

    def build_slots(slot_ids):
        hot = (slot_ids[:, None] == target[None, :]).astype(jnp.float32)
        values = jnp.dot(
            hot, block_values, precision=lax.Precision.HIGHEST, preferred_element_type=jnp.float32
        )
        filled = jnp.sum(hot, axis=1)
        keyed = jnp.sum(hot * local_keys[None, :], axis=1)
        keyed = jnp.where(filled > 0.5, keyed, jnp.float32(sentinel))
        return (values, keyed.astype(jnp.int32))

    slot_blocks = jnp.arange(slots_total, dtype=jnp.int32).reshape(
        slots_total // slot_step, slot_step
    )
    send_values, send_keys = lax.map(build_slots, slot_blocks)
    send_values = send_values.reshape(slots_total, TILE)
    send_keys = send_keys.reshape(slots_total)
    got_values, got_keys = (
        lax.all_to_all(
            send_values.reshape(devices_all, capacity, TILE),
            ("row", "col"),
            split_axis=0,
            concat_axis=0,
            tiled=True,
        ),
        lax.all_to_all(
            send_keys.reshape(devices_all, capacity),
            ("row", "col"),
            split_axis=0,
            concat_axis=0,
            tiled=True,
        ),
    )
    flat_values = got_values.reshape(slots_total, TILE)
    flat_keys = got_keys.reshape(slots_total)
    group = math.gcd(ROWS_DEV, 4)
    group_cells = group * tiles_count
    cell_ids = jnp.arange(group_cells, dtype=jnp.int32)

    def place_group(start):
        shifted = flat_keys - start * tiles_count
        hot = (cell_ids[:, None] == shifted[None, :]).astype(jnp.float32)
        placed = jnp.dot(
            hot, flat_values, precision=lax.Precision.HIGHEST, preferred_element_type=jnp.float32
        )
        return placed.reshape(group, tiles_count * TILE)

    starts = jnp.arange(0, ROWS_DEV, group, dtype=jnp.int32)
    summed = lax.map(place_group, starts).reshape(ROWS_DEV, tiles_count * TILE)
    rows_total = ROWS_DEV * devices_all
    block_row = owner * ROWS_DEV + block_offset
    tile_row = block_row // TILE
    row_hot = (
        jnp.arange(rows_total // TILE, dtype=jnp.int32)[:, None] == tile_row[None, :]
    ).astype(jnp.bfloat16)
    col_hot = (jnp.arange(tiles_count, dtype=jnp.int32)[:, None] == block_tiles[None, :]).astype(
        jnp.bfloat16
    )
    local_counts = lax.dot_general(
        row_hot, col_hot, (((1,), (1,)), ((), ())), preferred_element_type=jnp.float32
    ).astype(jnp.int32)
    occupancy = lax.psum(local_counts, ("row", "col"))
    return (summed, occupancy)


def solution(mesh):
    in_specs = (
        P(("row", "col"), None),
        P(("row", "col"), None),
        P(("row", "col")),
        P(("row", "col")),
    )
    out_specs = (P(("row", "col"), None), P())
    return jax.shard_map(body, mesh=mesh, in_specs=in_specs, out_specs=out_specs, check_vma=False)
```

profile of v0, /device:TPU:0, one launch (start us, length us, event | category | flops | bytes accessed | tf_op | source)
XLA Modules:
  0.0 188.5 jit_solution(14129278475890400826)
XLA Ops:
  0.7 2.3 %fusion.18 = f32[2048]{0:T(1024)S(1)} fusion(s32[2048]{0:T(1024)} %bitcast.29), kind=kOutput, calls=%fused_computation.21 | convolution fusion | flops 273020928 | bytes 16384 | tf_op jit(solution)/shard_map/dot_general | solution.py:28
  3.1 31.1 %while.23 = (s32[]{:T(128)}, f32[8,512,128]{2,1,0:T(8,128)}, s32[8,512]{1,0:T(8,128)S(1)}, s32[8,512]{1,0:T(8,128)S(1)}, s32[2048]{0:T(1024)S(1)}, /*index=5*/f3...) while((s32[]{:T(128)}, f32[8,512,128]{2,1,0:T(8,128)}, s32[8,512]{1,0:T(8,128)S(1)}, ...), condition=%wide.region_4.5_spmd, body=%wide.region_1.4_spmd.sunk | while | flops 1616904704 | bytes 1358437 | solution.py:47
  4.3 2.7 %fusion.35 = f32[8,512,128]{2,1,0:T(8,128)} fusion(f32[8,512,128]{2,1,0:T(8,128)} %get-tuple-element.204, s32[]{:T(128)} %get-tuple-element.203, f32[2048,128]{1,0:T(8,128)S(1)} %get-tuple-element.217, s32[2048]{0:T(1024)S(1)} %get-tuple-element.216, s32[512]{0:T(512)S(1)} %bitcast.28), kind=kOutput, calls=%fused_computation.10.clone.1 | convolution fusion | flops 1611661312 | bytes 1321472 | tf_op jit(solution)/shard_map/while/body/eval_jaxpr/dot_general | solution.py:36
  8.2 2.7 %fusion.35 = f32[8,512,128]{2,1,0:T(8,128)} fusion(f32[8,512,128]{2,1,0:T(8,128)} %get-tuple-element.204, s32[]{:T(128)} %get-tuple-element.203, f32[2048,128]{1,0:T(8,128)S(1)} %get-tuple-element.217, s32[2048]{0:T(1024)S(1)} %get-tuple-element.216, s32[512]{0:T(512)S(1)} %bitcast.28), kind=kOutput, calls=%fused_computation.10.clone.1 | convolution fusion | flops 1611661312 | bytes 1321472 | tf_op jit(solution)/shard_map/while/body/eval_jaxpr/dot_general | solution.py:36
  12.1 2.7 %fusion.35 = f32[8,512,128]{2,1,0:T(8,128)} fusion(f32[8,512,128]{2,1,0:T(8,128)} %get-tuple-element.204, s32[]{:T(128)} %get-tuple-element.203, f32[2048,128]{1,0:T(8,128)S(1)} %get-tuple-element.217, s32[2048]{0:T(1024)S(1)} %get-tuple-element.216, s32[512]{0:T(512)S(1)} %bitcast.28), kind=kOutput, calls=%fused_computation.10.clone.1 | convolution fusion | flops 1611661312 | bytes 1321472 | tf_op jit(solution)/shard_map/while/body/eval_jaxpr/dot_general | solution.py:36
  15.9 2.7 %fusion.35 = f32[8,512,128]{2,1,0:T(8,128)} fusion(f32[8,512,128]{2,1,0:T(8,128)} %get-tuple-element.204, s32[]{:T(128)} %get-tuple-element.203, f32[2048,128]{1,0:T(8,128)S(1)} %get-tuple-element.217, s32[2048]{0:T(1024)S(1)} %get-tuple-element.216, s32[512]{0:T(512)S(1)} %bitcast.28), kind=kOutput, calls=%fused_computation.10.clone.1 | convolution fusion | flops 1611661312 | bytes 1321472 | tf_op jit(solution)/shard_map/while/body/eval_jaxpr/dot_general | solution.py:36
  19.8 2.7 %fusion.35 = f32[8,512,128]{2,1,0:T(8,128)} fusion(f32[8,512,128]{2,1,0:T(8,128)} %get-tuple-element.204, s32[]{:T(128)} %get-tuple-element.203, f32[2048,128]{1,0:T(8,128)S(1)} %get-tuple-element.217, s32[2048]{0:T(1024)S(1)} %get-tuple-element.216, s32[512]{0:T(512)S(1)} %bitcast.28), kind=kOutput, calls=%fused_computation.10.clone.1 | convolution fusion | flops 1611661312 | bytes 1321472 | tf_op jit(solution)/shard_map/while/body/eval_jaxpr/dot_general | solution.py:36
  23.7 2.7 %fusion.35 = f32[8,512,128]{2,1,0:T(8,128)} fusion(f32[8,512,128]{2,1,0:T(8,128)} %get-tuple-element.204, s32[]{:T(128)} %get-tuple-element.203, f32[2048,128]{1,0:T(8,128)S(1)} %get-tuple-element.217, s32[2048]{0:T(1024)S(1)} %get-tuple-element.216, s32[512]{0:T(512)S(1)} %bitcast.28), kind=kOutput, calls=%fused_computation.10.clone.1 | convolution fusion | flops 1611661312 | bytes 1321472 | tf_op jit(solution)/shard_map/while/body/eval_jaxpr/dot_general | solution.py:36
  27.6 2.7 %fusion.35 = f32[8,512,128]{2,1,0:T(8,128)} fusion(f32[8,512,128]{2,1,0:T(8,128)} %get-tuple-element.204, s32[]{:T(128)} %get-tuple-element.203, f32[2048,128]{1,0:T(8,128)S(1)} %get-tuple-element.217, s32[2048]{0:T(1024)S(1)} %get-tuple-element.216, s32[512]{0:T(512)S(1)} %bitcast.28), kind=kOutput, calls=%fused_computation.10.clone.1 | convolution fusion | flops 1611661312 | bytes 1321472 | tf_op jit(solution)/shard_map/while/body/eval_jaxpr/dot_general | solution.py:36
  31.5 2.7 %fusion.35 = f32[8,512,128]{2,1,0:T(8,128)} fusion(f32[8,512,128]{2,1,0:T(8,128)} %get-tuple-element.204, s32[]{:T(128)} %get-tuple-element.203, f32[2048,128]{1,0:T(8,128)S(1)} %get-tuple-element.217, s32[2048]{0:T(1024)S(1)} %get-tuple-element.216, s32[512]{0:T(512)S(1)} %bitcast.28), kind=kOutput, calls=%fused_computation.10.clone.1 | convolution fusion | flops 1611661312 | bytes 1321472 | tf_op jit(solution)/shard_map/while/body/eval_jaxpr/dot_general | solution.py:36
  34.2 14.3 %all_to_all.14 = s32[32,1,128]{2,1,0:T(1,128)S(1)} all-to-all(s32[32,1,128]{2,1,0:T(1,128)S(1)} %all_to_all.9), channel_id=1, replica_groups=mesh['row'=4,'col'=8] {'row','col'}, dimensions={0} | all-to-all | bytes 32768 | tf_op jit(solution)/shard_map/all_to_all | solution.py:58
  48.5 3.5 %all-to-all-start.1 = ((f32[32,128,128]{2,1,0:T(8,128)}), f32[32,128,128]{2,1,0:T(8,128)}, u32[]{:S(2)}, u32[]{:S(2)}) async-start(f32[32,128,128]{2,1,0:T(8,128)} %bitcast.5), calls=%async_computation.1 | async-start | bytes 4194304 | tf_op jit(solution)/shard_map/all_to_all | solution.py:51
  52.2 68.9 %psum.7 = s32[10,108]{1,0:T(8,128)} all-reduce(s32[10,108]{1,0:T(8,128)S(1)} %convolution_convert_fusion), channel_id=1, replica_groups=mesh['row'=4,'col'=8] {'row','col'}, use_global_device_ids=true, to_apply=%region_7.8 | all-reduce | flops 1080 | bytes 8640 | tf_op jit(solution)/shard_map/psum | solution.py:94
  121.2 65.2 %while.24 = (s32[]{:T(128)}, f32[10,4,13824]{2,1,0:T(4,128)S(1)}, s32[10]{0:T(128)S(1)}, s32[4096]{0:T(1024)S(1)}, f32[4096,128]{1,0:T(8,128)}, /*index=5*/s32[]{:T(128)}, s32[1]{0:T(128)}) while((s32[]{:T(128)}, f32[10,4,13824]{2,1,0:T(4,128)S(1)}, s32[10]{0:T(128)S(1)}, s32[4096]{0:T(1024)S(1)}, f32[4096,128]{1,0:T(8,128)}, ...), condition=%wide.region_6.7_spmd.clone, body=%wide.region_5.6_spmd.clone.sunk | while | flops 2719682560 | bytes 3252333 | solution.py:81
  122.4 5.1 %fusion.38 = f32[432,128]{1,0:T(8,128)S(1)} fusion(f32[4096,128]{1,0:T(8,128)} %get-tuple-element.239, s32[4096]{0:T(1024)S(1)} %broadcast_subtract_fusion.2), kind=kOutput, calls=%fused_computation.14.clone.1 | convolution fusion | flops 2719678464 | bytes 2334720 | tf_op jit(solution)/shard_map/while/body/eval_jaxpr/dot_general | solution.py:75
  128.9 5.1 %fusion.38 = f32[432,128]{1,0:T(8,128)S(1)} fusion(f32[4096,128]{1,0:T(8,128)} %get-tuple-element.239, s32[4096]{0:T(1024)S(1)} %broadcast_subtract_fusion.2), kind=kOutput, calls=%fused_computation.14.clone.1 | convolution fusion | flops 2719678464 | bytes 2334720 | tf_op jit(solution)/shard_map/while/body/eval_jaxpr/dot_general | solution.py:75
  135.4 5.1 %fusion.38 = f32[432,128]{1,0:T(8,128)S(1)} fusion(f32[4096,128]{1,0:T(8,128)} %get-tuple-element.239, s32[4096]{0:T(1024)S(1)} %broadcast_subtract_fusion.2), kind=kOutput, calls=%fused_computation.14.clone.1 | convolution fusion | flops 2719678464 | bytes 2334720 | tf_op jit(solution)/shard_map/while/body/eval_jaxpr/dot_general | solution.py:75
  142.0 5.1 %fusion.38 = f32[432,128]{1,0:T(8,128)S(1)} fusion(f32[4096,128]{1,0:T(8,128)} %get-tuple-element.239, s32[4096]{0:T(1024)S(1)} %broadcast_subtract_fusion.2), kind=kOutput, calls=%fused_computation.14.clone.1 | convolution fusion | flops 2719678464 | bytes 2334720 | tf_op jit(solution)/shard_map/while/body/eval_jaxpr/dot_general | solution.py:75
  148.5 5.1 %fusion.38 = f32[432,128]{1,0:T(8,128)S(1)} fusion(f32[4096,128]{1,0:T(8,128)} %get-tuple-element.239, s32[4096]{0:T(1024)S(1)} %broadcast_subtract_fusion.2), kind=kOutput, calls=%fused_computation.14.clone.1 | convolution fusion | flops 2719678464 | bytes 2334720 | tf_op jit(solution)/shard_map/while/body/eval_jaxpr/dot_general | solution.py:75
  155.0 5.1 %fusion.38 = f32[432,128]{1,0:T(8,128)S(1)} fusion(f32[4096,128]{1,0:T(8,128)} %get-tuple-element.239, s32[4096]{0:T(1024)S(1)} %broadcast_subtract_fusion.2), kind=kOutput, calls=%fused_computation.14.clone.1 | convolution fusion | flops 2719678464 | bytes 2334720 | tf_op jit(solution)/shard_map/while/body/eval_jaxpr/dot_general | solution.py:75
  161.5 5.1 %fusion.38 = f32[432,128]{1,0:T(8,128)S(1)} fusion(f32[4096,128]{1,0:T(8,128)} %get-tuple-element.239, s32[4096]{0:T(1024)S(1)} %broadcast_subtract_fusion.2), kind=kOutput, calls=%fused_computation.14.clone.1 | convolution fusion | flops 2719678464 | bytes 2334720 | tf_op jit(solution)/shard_map/while/body/eval_jaxpr/dot_general | solution.py:75
  168.0 5.1 %fusion.38 = f32[432,128]{1,0:T(8,128)S(1)} fusion(f32[4096,128]{1,0:T(8,128)} %get-tuple-element.239, s32[4096]{0:T(1024)S(1)} %broadcast_subtract_fusion.2), kind=kOutput, calls=%fused_computation.14.clone.1 | convolution fusion | flops 2719678464 | bytes 2334720 | tf_op jit(solution)/shard_map/while/body/eval_jaxpr/dot_general | solution.py:75
  174.6 5.1 %fusion.38 = f32[432,128]{1,0:T(8,128)S(1)} fusion(f32[4096,128]{1,0:T(8,128)} %get-tuple-element.239, s32[4096]{0:T(1024)S(1)} %broadcast_subtract_fusion.2), kind=kOutput, calls=%fused_computation.14.clone.1 | convolution fusion | flops 2719678464 | bytes 2334720 | tf_op jit(solution)/shard_map/while/body/eval_jaxpr/dot_general | solution.py:75
  181.1 5.1 %fusion.38 = f32[432,128]{1,0:T(8,128)S(1)} fusion(f32[4096,128]{1,0:T(8,128)} %get-tuple-element.239, s32[4096]{0:T(1024)S(1)} %broadcast_subtract_fusion.2), kind=kOutput, calls=%fused_computation.14.clone.1 | convolution fusion | flops 2719678464 | bytes 2334720 | tf_op jit(solution)/shard_map/while/body/eval_jaxpr/dot_general | solution.py:75
  (90 shorter events, 19.1 us)
Async XLA Ops:
  0.7 2.4 %copy-start = (s32[2048]{0:T(1024)S(1)}, s32[2048]{0:T(1024)}, u32[]{:S(2)}) copy-start(s32[2048]{0:T(1024)} %param.10) | copy-start | bytes 24580
  0.7 2.4 %copy-start.1 = (s32[2048,1]{0,1:T(1,128)S(1)}, s32[2048,1]{0,1:T(1,128)}, u32[]{:S(2)}) copy-start(s32[2048,1]{0,1:T(1,128)} %param.9) | copy-start | bytes 24580
  0.7 2.4 %copy-start.2 = (s32[2048]{0:T(1024)S(1)}, s32[2048]{0:T(1024)}, u32[]{:S(2)}) copy-start(s32[2048]{0:T(1024)} %param.11) | copy-start | bytes 24580
  0.7 2.4 %copy-start.3 = (f32[2048,128]{1,0:T(8,128)S(1)}, f32[2048,128]{1,0:T(8,128)}, u32[]{:S(2)}) copy-start(f32[2048,128]{1,0:T(8,128)} %param.8) | copy-start | bytes 3145732
  48.5 72.7 %all-to-all-start.1 = ((f32[32,128,128]{2,1,0:T(8,128)}), f32[32,128,128]{2,1,0:T(8,128)}, u32[]{:S(2)}, u32[]{:S(2)}) async-start(f32[32,128,128]{2,1,0:T(8,128)} %bitcast.5), calls=%async_computation.1 | async-start | bytes 4194304 | tf_op jit(solution)/shard_map/all_to_all | solution.py:51
where the time goes:
time: 189 us; the launch traced here: 188 us
  blocking collectives  83.2 us (44%)
  matrix products  75.1 us (40%)
  local copies, waits for them, and re-layouts  9.82 us (5%)
  other arithmetic  9.05 us (5%)
  loops' own time  7.08 us (4%)
  starting transfers between devices  3.48 us (2%)
    psum x1, blocking collectives, body(): occupancy = lax.psum(local_counts, ('row', 'col'))  68.9 us
    dot_general x10, matrix products, place_group(): jnp.dot(hot, flat_values, precision=lax.Precision.HIGHEST, preferred_elem...  51.1 us
    dot_general x8, matrix products, build_slots(): jnp.dot(hot, block_values, precision=lax.Precision.HIGHEST, preferred_ele...  21.4 us
    all_to_all x1, blocking collectives, body(): lax.all_to_all(send_keys.reshape(devices_all, capacity), ('row', 'col'),...  14.3 us
    reduce_sum x8, other arithmetic, build_slots(): filled = jnp.sum(hot, axis=1)  8.91 us
    another operation x1, loops' own time, body(): summed = lax.map(place_group, starts).reshape(ROWS_DEV, tiles_count * TILE)  6.97 us
    dynamic_slice x10, local copies, waits for them, and re-layouts, body(): summed = lax.map(place_group, starts).reshape(ROWS_DEV, tiles_count * TILE)  5.86 us
  transfers between devices with their start and end apart: 1, of which 0 were waited for; matrix products, arithmetic and copies ran while one was open for 0% of the time, Pallas kernels for 0%

commit v1 on v0

v1 whole, which is shorter than its diff:
```python
import functools
import math

import jax
import jax.numpy as jnp
from jax import lax
from jax.experimental import pallas as pl
from jax.experimental.pallas import tpu as pltpu
from jax.sharding import PartitionSpec as P

F = 13824
TILE = 128
ROWS_DEV = 40
SUB = 8
MESH = pl.DeviceIdType.MESH
CHAINS = 4


def spread_kernel(capacity, target_ref, key_ref, fill_ref, values_ref, send_ref, keys_ref, sem):
    fill = pltpu.make_async_copy(fill_ref, keys_ref, sem)
    fill.start()
    fill.wait()
    step = math.gcd(values_ref.shape[0], 16)

    def group(g, carry):
        base = pl.multiple_of(g * step, step)
        for i in range(step):
            t = target_ref[base + i]
            send_ref[pl.ds(t, 1), :] = values_ref[pl.ds(base + i, 1), :]
            keys_ref[t // capacity, 0, t % capacity] = key_ref[base + i]
        return carry

    lax.fori_loop(0, values_ref.shape[0] // step, group, 0)


def exchange_kernel(
    rows,
    cols,
    send_ref,
    keys_ref,
    counts_ref,
    got_ref,
    got_keys_ref,
    total_ref,
    plane,
    every,
    own,
    val_send,
    val_recv,
    key_send,
    key_recv,
    plane_send,
    plane_recv,
    every_send,
    every_recv,
    local_sem,
):
    r, c = lax.axis_index("row"), lax.axis_index("col")
    me = r * cols + c
    n = rows * cols
    barrier = pltpu.get_barrier_semaphore()

    def greet(k, carry):
        to = lax.rem(me + k, n)
        pl.semaphore_signal(
            barrier, inc=1, device_id=(to // cols, lax.rem(to, cols)), device_id_type=MESH
        )
        return carry

    lax.fori_loop(1, n, greet, 0)
    pl.semaphore_wait(barrier, n - 1)

    def plane_copy(k):
        return pltpu.make_async_remote_copy(
            src_ref=counts_ref,
            dst_ref=plane.at[r],
            send_sem=plane_send.at[k],
            recv_sem=plane_recv.at[k],
            device_id=(lax.rem(r + k, rows), c),
            device_id_type=MESH,
        )

    def every_copy(k):
        return pltpu.make_async_remote_copy(
            src_ref=plane,
            dst_ref=every.at[c],
            send_sem=every_send.at[k],
            recv_sem=every_recv.at[k],
            device_id=(r, lax.rem(c + k, cols)),
            device_id_type=MESH,
        )

    def value_copies(k):
        to_row, to_col = lax.rem(r + k // cols, rows), lax.rem(c + lax.rem(k, cols), cols)
        to = to_row * cols + to_col
        where = dict(device_id=(to_row, to_col), device_id_type=MESH)
        return (
            pltpu.make_async_remote_copy(
                src_ref=keys_ref.at[to],
                dst_ref=got_keys_ref.at[me],
                send_sem=key_send.at[k],
                recv_sem=key_recv.at[k],
                **where,
            ),
            pltpu.make_async_remote_copy(
                src_ref=send_ref.at[to],
                dst_ref=got_ref.at[me],
                send_sem=val_send.at[k],
                recv_sem=val_recv.at[k],
                **where,
            ),
        )

    for k in range(1, rows):
        plane_copy(k).start()

    def start_all(low, high):
        def one(k, carry):
            for copy in value_copies(k):
                copy.start()
            return carry

        lax.fori_loop(low, high, one, 0)

    order = sorted(range(rows), key=lambda d: -min(d, rows - d))
    for d in order:
        start_all(max(d * cols, 1), (d + 1) * cols)
    own_in = pltpu.make_async_copy(send_ref.at[me], own, local_sem.at[0])
    own_in.start()
    own_keys = pltpu.make_async_copy(keys_ref.at[me], got_keys_ref.at[me], local_sem.at[1])
    own_keys.start()
    own_counts = pltpu.make_async_copy(counts_ref, plane.at[r], local_sem.at[2])
    own_counts.start()
    own_in.wait()
    own_out = pltpu.make_async_copy(own, got_ref.at[me], local_sem.at[0])
    own_out.start()
    own_counts.wait()
    for k in range(1, rows):
        plane_copy(k).wait()

    def start_every(k, carry):
        every_copy(k).start()
        return carry

    lax.fori_loop(1, cols, start_every, 0)
    own_keys.wait()
    own_out.wait()

    def wait_all(k, carry):
        for copy in value_copies(k):
            copy.wait()
        return carry

    lax.fori_loop(1, n, wait_all, 0)

    def wait_every(k, carry):
        every_copy(k).wait()
        return carry

    lax.fori_loop(1, cols, wait_every, 0)
    mine = plane[0]
    for i in range(1, rows):
        mine = mine + plane[i]
    total_ref[...] = mine

    def add_every(k, carry):
        other = lax.rem(c + k, cols)
        for i in range(rows):
            total_ref[...] += every[other, i]
        return carry

    lax.fori_loop(1, cols, add_every, 0)


def place_kernel(keys_ref, values_ref, out_ref, *rest):
    accs, (outbuf, sems) = rest[:CHAINS], rest[CHAINS:]
    step = pl.program_id(0)
    sources, _, capacity = keys_ref.shape
    cells = accs[0].shape[0] - SUB
    tiles = cells // ROWS_DEV
    unit = math.gcd(capacity, 32)

    @pl.when(step == 0)
    def _():
        for acc in accs:
            acc[...] = jnp.zeros_like(acc)

    def source(s, carry):
        def group(g, carry):
            base = pl.multiple_of(g * unit, unit)
            row = pl.multiple_of(s * capacity + base, unit)
            for j in range(0, unit, CHAINS):
                at = [keys_ref[s, 0, base + j + q] for q in range(CHAINS)]
                sums = [
                    accs[q][pl.ds(at[q], 1), :] + values_ref[pl.ds(row + j + q, 1), :]
                    for q in range(CHAINS)
                ]
                for q in range(CHAINS):
                    accs[q][pl.ds(at[q], 1), :] = sums[q]
            return carry

        return lax.fori_loop(0, capacity // unit, group, carry)

    lax.fori_loop(0, sources, source, 0)

    @pl.when(step == pl.num_programs(0) - 1)
    def _():
        copies = []
        for g in range(ROWS_DEV // SUB):
            for c in range(tiles):
                at = pl.ds((g * tiles + c) * SUB, SUB)
                total = accs[0][at, :]
                for acc in accs[1:]:
                    total = total + acc[at, :]
                outbuf[g * SUB : (g + 1) * SUB, c * TILE : (c + 1) * TILE] = total
            rows = pl.ds(g * SUB, SUB)
            copy = pltpu.make_async_copy(outbuf.at[rows], out_ref.at[rows], sems.at[g])
            copy.start()
            copies.append(copy)
        for copy in copies:
            copy.wait()


def body(block_values, block_owner, block_offset, block_tiles):
    tiles_count = F // TILE
    size_row = lax.axis_size("row")
    size_col = lax.axis_size("col")
    devices_all = size_row * size_col
    local_blocks = block_values.shape[0]
    capacity = 2 * local_blocks // devices_all
    slots_total = devices_all * capacity
    owner = block_owner[:, 0]
    cells = ROWS_DEV * tiles_count
    owner_hot = (owner[:, None] == jnp.arange(devices_all, dtype=jnp.int32)[None, :]).astype(
        jnp.bfloat16
    )
    positions = jnp.arange(local_blocks, dtype=jnp.int32)
    earlier = (positions[None, :] < positions[:, None]).astype(jnp.bfloat16)
    before = jnp.dot(earlier, owner_hot, preferred_element_type=jnp.float32)
    slot = jnp.sum(before * owner_hot.astype(jnp.float32), axis=1).astype(jnp.int32)
    target = owner * capacity + slot
    local_keys = (block_offset // SUB * tiles_count + block_tiles) * SUB + block_offset % SUB

    vmem, smem, anywhere = (
        pl.BlockSpec(memory_space=m) for m in (pltpu.VMEM, pltpu.SMEM, pl.ANY)
    )
    fill = jnp.full((devices_all, 1, capacity), cells, jnp.int32)
    send, send_keys = pl.pallas_call(
        functools.partial(spread_kernel, capacity),
        out_shape=(
            jax.ShapeDtypeStruct((slots_total, TILE), jnp.float32),
            jax.ShapeDtypeStruct((devices_all, 1, capacity), jnp.int32),
        ),
        in_specs=[smem, smem, anywhere, vmem],
        out_specs=(vmem, smem),
        scratch_shapes=[pltpu.SemaphoreType.DMA],
        name="spread",
    )(target, local_keys, fill, block_values)

    rows_total = ROWS_DEV * devices_all
    tile_rows = rows_total // TILE
    block_row = owner * ROWS_DEV + block_offset
    tile_row = block_row // TILE
    row_hot = (jnp.arange(tile_rows, dtype=jnp.int32)[:, None] == tile_row[None, :]).astype(
        jnp.bfloat16
    )
    col_hot = (jnp.arange(TILE, dtype=jnp.int32)[:, None] == block_tiles[None, :]).astype(
        jnp.bfloat16
    )
    local_counts = lax.dot_general(
        row_hot, col_hot, (((1,), (1,)), ((), ())), preferred_element_type=jnp.float32
    ).astype(jnp.int32)

    sems = pltpu.SemaphoreType.DMA
    got, got_keys, total = pl.pallas_call(
        functools.partial(exchange_kernel, size_row, size_col),
        out_shape=(
            jax.ShapeDtypeStruct((devices_all, capacity, TILE), jnp.float32),
            jax.ShapeDtypeStruct((devices_all, 1, capacity), jnp.int32),
            jax.ShapeDtypeStruct((tile_rows, TILE), jnp.int32),
        ),
        in_specs=[anywhere, anywhere, anywhere],
        out_specs=(anywhere, anywhere, vmem),
        scratch_shapes=[
            pltpu.VMEM((size_row, tile_rows, TILE), jnp.int32),
            pltpu.VMEM((size_col, size_row, tile_rows, TILE), jnp.int32),
            pltpu.VMEM((capacity, TILE), jnp.float32),
            sems((devices_all,)),
            sems((devices_all,)),
            sems((devices_all,)),
            sems((devices_all,)),
            sems((size_row,)),
            sems((size_row,)),
            sems((size_col,)),
            sems((size_col,)),
            sems((3,)),
        ],
        compiler_params=pltpu.CompilerParams(collective_id=0, has_side_effects=True),
        name="exchange",
    )(send.reshape(devices_all, capacity, TILE), send_keys, local_counts)

    batch = math.gcd(devices_all, 4)
    summed = pl.pallas_call(
        place_kernel,
        out_shape=jax.ShapeDtypeStruct((ROWS_DEV, F), jnp.float32),
        grid=(devices_all // batch,),
        in_specs=[
            pl.BlockSpec((batch, 1, capacity), lambda i: (i, 0, 0), memory_space=pltpu.SMEM),
            pl.BlockSpec((batch * capacity, TILE), lambda i: (i, 0)),
        ],
        out_specs=anywhere,
        scratch_shapes=[pltpu.VMEM((cells + SUB, TILE), jnp.float32)] * CHAINS
        + [pltpu.VMEM((ROWS_DEV, F), jnp.float32), sems((ROWS_DEV // SUB,))],
        name="place",
    )(got_keys, got.reshape(slots_total, TILE))
    return (summed, total[:, :tiles_count])


def solution(mesh):
    in_specs = (
        P(("row", "col"), None),
        P(("row", "col"), None),
        P(("row", "col")),
        P(("row", "col")),
    )
    out_specs = (P(("row", "col"), None), P())
    return jax.shard_map(body, mesh=mesh, in_specs=in_specs, out_specs=out_specs, check_vma=False)
```

time: 189 us -> 93.9 us (0.50)
  the two profiles are of different devices: /device:TPU:0 before, /device:TPU:11 now
where the time goes in v1:
time: 93.9 us; the launch traced here: 93.5 us
  Pallas kernels  87.8 us (94%)
  matrix products  3.15 us (3%)
  local copies, waits for them, and re-layouts  1.22 us (1%)
    pallas_call x1, Pallas kernels, body(): pl.pallas_call(functools.partial(exchange_kernel, size_row, size_col), ou...  54.7 us
    pallas_call x1, Pallas kernels, body(): pl.pallas_call(functools.partial(spread_kernel, capacity), out_shape=(jax...  20.3 us
    pallas_call x1, Pallas kernels, body(): pl.pallas_call(place_kernel, out_shape=jax.ShapeDtypeStruct((ROWS_DEV, F)...  12.8 us
    dot_general x1, matrix products, body(): before = jnp.dot(earlier, owner_hot, preferred_element_type=jnp.float32)  2.27 us

profile of v1, /device:TPU:11, one launch (start us, length us, event | category | flops | bytes accessed | tf_op | source)
XLA Modules:
  0.0 93.5 jit_solution(14546923332293987835)
XLA Ops:
  0.6 0.0 copy-start
  0.6 0.0 copy-start.1
  0.7 0.0 copy-start.2
  0.7 2.3 %fusion.2 = f32[2048]{0:T(1024)S(1)} fusion(s32[2048]{0:T(1024)} %bitcast.6), kind=kOutput, calls=%fused_computation.3 | convolution fusion | flops 273020928 | bytes 16384 | tf_op jit(solution)/shard_map/dot_general | solution.py:239
  2.9 0.0 copy-done
  3.0 0.0 copy-done.1
  3.0 0.0 copy-done.2
  3.0 0.6 add_select_fusion
  3.6 0.9 convolution_convert_fusion.counts_ref
  4.5 0.6 broadcast_in_dim.2.fill_ref
  5.1 20.3 %spread.1 = (f32[4096,128]{1,0:T(8,128)}, s32[32,1,128]{2,1,0:T(1,128)}) custom-call(s32[2048]{0:T(1024)} %get-tuple-element.13.target_ref, s32[2048]{0:T(1024)} %get-tuple-element.14.key_ref, s32[32,1,128]{2,1,0:T(1,128)} %broadcast_in_dim.2.fill_ref, f32[2048,128]{1,0:T(8,128)} %values_ref.1), custom_call_target="tpu_custom_call" | custom-call | tf_op jit(solution)/shard_map/spread/pallas_call | solution.py:248
  25.4 54.7 %exchange.1 = (f32[32,128,128]{2,1,0:T(8,128)}, s32[32,1,128]{2,1,0:T(1,128)}, s32[10,128]{1,0:T(8,128)}) custom-call(f32[32,128,128]{2,1,0:T(8,128)} %bitcast.4, s32[32,1,128]{2,1,0:T(1,128)} %get-tuple-element.8.keys_ref, s32[10,128]{1,0:T(8,128)} %convolution_convert_fusion.counts_ref), custom_call_target="tpu_custom_call" | custom-call | tf_op jit(solution)/shard_map/exchange/pallas_call | solution.py:275
  80.1 0.0 copy-start.3
  80.1 12.8 %place.1 = f32[40,13824]{1,0:T(8,128)} custom-call(s32[32,1,128]{2,1,0:T(1,128)} %get-tuple-element.9.keys_ref, f32[4096,128]{1,0:T(8,128)} %bitcast.5), custom_call_target="tpu_custom_call" | custom-call | tf_op jit(solution)/shard_map/place/pallas_call | solution.py:303
  92.9 0.0 copy-done.3
  92.9 0.6 copy.7
Async XLA Ops:
  0.6 2.3 %copy-start = (s32[2048]{0:T(1024)S(1)}, s32[2048]{0:T(1024)}, u32[]{:S(2)}) copy-start(s32[2048]{0:T(1024)} %param.6) | copy-start | bytes 24580
  0.6 2.3 %copy-start.1 = (s32[2048,1]{0,1:T(1,128)S(1)}, s32[2048,1]{0,1:T(1,128)}, u32[]{:S(2)}) copy-start(s32[2048,1]{0,1:T(1,128)} %param.5) | copy-start | bytes 24580
  0.7 2.3 %copy-start.2 = (s32[2048]{0:T(1024)S(1)}, s32[2048]{0:T(1024)}, u32[]{:S(2)}) copy-start(s32[2048]{0:T(1024)} %param.7) | copy-start | bytes 24580
  80.1 12.8 %copy-start.3 = (s32[10,128]{1,0:T(8,128)S(1)}, s32[10,128]{1,0:T(8,128)}, u32[]{:S(2)}) copy-start(s32[10,128]{1,0:T(8,128)} %get-tuple-element.11) | copy-start | bytes 15364

commit v2 on v1

--- a/solution.py
+++ b/solution.py
@@ -16,7 +16,7 @@
 CHAINS = 4
 
 
-def spread_kernel(capacity, target_ref, key_ref, fill_ref, values_ref, send_ref, keys_ref, sem):
+def spread_kernel(target_ref, key_ref, fill_ref, values_ref, send_ref, keys_ref, sem):
     fill = pltpu.make_async_copy(fill_ref, keys_ref, sem)
     fill.start()
     fill.wait()
@@ -24,10 +24,12 @@
 
     def group(g, carry):
         base = pl.multiple_of(g * step, step)
+        to = [target_ref[base + i] for i in range(step)]
+        keys = [key_ref[base + i] for i in range(step)]
         for i in range(step):
-            t = target_ref[base + i]
-            send_ref[pl.ds(t, 1), :] = values_ref[pl.ds(base + i, 1), :]
-            keys_ref[t // capacity, 0, t % capacity] = key_ref[base + i]
+            send_ref[pl.ds(to[i], 1), :] = values_ref[pl.ds(base + i, 1), :]
+        for i in range(step):
+            keys_ref[to[i]] = keys[i]
         return carry
 
     lax.fori_loop(0, values_ref.shape[0] // step, group, 0)
@@ -60,6 +62,20 @@
     n = rows * cols
     barrier = pltpu.get_barrier_semaphore()
 
+    paired = rows & (rows - 1) == 0
+    order = [rows // 2] + [d for d in range(1, rows) if d != rows // 2] + [0]
+
+    def partner(at, d):
+        if not paired:
+            return lax.rem(at + d, rows)
+        out, bit = at, 1
+        while bit < rows:
+            if d & bit:
+                half = lax.rem(out // bit, 2)
+                out = out + bit - 2 * bit * half
+            bit *= 2
+        return out
+
     def greet(k, carry):
         to = lax.rem(me + k, n)
         pl.semaphore_signal(
@@ -90,8 +106,9 @@
             device_id_type=MESH,
         )
 
-    def value_copies(k):
-        to_row, to_col = lax.rem(r + k // cols, rows), lax.rem(c + lax.rem(k, cols), cols)
+    def value_copies(d, e):
+        k = d * cols + e
+        to_row, to_col = partner(r, d), lax.rem(c + e, cols)
         to = to_row * cols + to_col
         where = dict(device_id=(to_row, to_col), device_id_type=MESH)
         return (
@@ -114,17 +131,17 @@
     for k in range(1, rows):
         plane_copy(k).start()
 
-    def start_all(low, high):
-        def one(k, carry):
-            for copy in value_copies(k):
-                copy.start()
-            return carry
-
-        lax.fori_loop(low, high, one, 0)
-
-    order = sorted(range(rows), key=lambda d: -min(d, rows - d))
-    for d in order:
-        start_all(max(d * cols, 1), (d + 1) * cols)
+    def for_all(act):
+        for d in order:
+
+            def one(e, carry):
+                for copy in value_copies(d, e):
+                    act(copy)
+                return carry
+
+            lax.fori_loop(0 if d else 1, cols, one, 0)
+
+    for_all(lambda copy: copy.start())
     own_in = pltpu.make_async_copy(send_ref.at[me], own, local_sem.at[0])
     own_in.start()
     own_keys = pltpu.make_async_copy(keys_ref.at[me], got_keys_ref.at[me], local_sem.at[1])
@@ -146,12 +163,7 @@
     own_keys.wait()
     own_out.wait()
 
-    def wait_all(k, carry):
-        for copy in value_copies(k):
-            copy.wait()
-        return carry
-
-    lax.fori_loop(1, n, wait_all, 0)
+    for_all(lambda copy: copy.wait())
 
     def wait_every(k, carry):
         every_copy(k).wait()
@@ -189,14 +201,14 @@
         def group(g, carry):
             base = pl.multiple_of(g * unit, unit)
             row = pl.multiple_of(s * capacity + base, unit)
+            at = [keys_ref[s, 0, base + j] for j in range(unit)]
             for j in range(0, unit, CHAINS):
-                at = [keys_ref[s, 0, base + j + q] for q in range(CHAINS)]
                 sums = [
-                    accs[q][pl.ds(at[q], 1), :] + values_ref[pl.ds(row + j + q, 1), :]
+                    accs[q][pl.ds(at[j + q], 1), :] + values_ref[pl.ds(row + j + q, 1), :]
                     for q in range(CHAINS)
                 ]
                 for q in range(CHAINS):
-                    accs[q][pl.ds(at[q], 1), :] = sums[q]
+                    accs[q][pl.ds(at[j + q], 1), :] = sums[q]
             return carry
 
         return lax.fori_loop(0, capacity // unit, group, carry)
@@ -244,12 +256,12 @@
     vmem, smem, anywhere = (
         pl.BlockSpec(memory_space=m) for m in (pltpu.VMEM, pltpu.SMEM, pl.ANY)
     )
-    fill = jnp.full((devices_all, 1, capacity), cells, jnp.int32)
+    fill = jnp.full((slots_total,), cells, jnp.int32)
     send, send_keys = pl.pallas_call(
-        functools.partial(spread_kernel, capacity),
+        spread_kernel,
         out_shape=(
             jax.ShapeDtypeStruct((slots_total, TILE), jnp.float32),
-            jax.ShapeDtypeStruct((devices_all, 1, capacity), jnp.int32),
+            jax.ShapeDtypeStruct((slots_total,), jnp.int32),
         ),
         in_specs=[smem, smem, anywhere, vmem],
         out_specs=(vmem, smem),
@@ -297,7 +309,11 @@
         ],
         compiler_params=pltpu.CompilerParams(collective_id=0, has_side_effects=True),
         name="exchange",
-    )(send.reshape(devices_all, capacity, TILE), send_keys, local_counts)
+    )(
+        send.reshape(devices_all, capacity, TILE),
+        send_keys.reshape(devices_all, 1, capacity),
+        local_counts,
+    )
 
     batch = math.gcd(devices_all, 4)
     summed = pl.pallas_call(

time: 93.9 us -> 82.2 us (0.88)
  Pallas kernels: 87.8 us -> 76.1 us
    pallas_call x1, Pallas kernels: 20.3 us -> 7.13 us  [body(): pl.pallas_call(spread_kernel, out_shape=(jax.ShapeDtypeStruct((slots_tota...]
    pallas_call x1, Pallas kernels: 12.8 us -> 14.2 us  [body(): pl.pallas_call(place_kernel, out_shape=jax.ShapeDtypeStruct((ROWS_DEV, F)...]
where the time goes in v2:
time: 82.2 us; the launch traced here: 81.8 us
  Pallas kernels  76.1 us (93%)
  matrix products  3.15 us (4%)
  local copies, waits for them, and re-layouts  1.22 us (1%)
    pallas_call x1, Pallas kernels, body(): pl.pallas_call(functools.partial(exchange_kernel, size_row, size_col), ou...  54.8 us
    pallas_call x1, Pallas kernels, body(): pl.pallas_call(place_kernel, out_shape=jax.ShapeDtypeStruct((ROWS_DEV, F)...  14.2 us
    pallas_call x1, Pallas kernels, body(): pl.pallas_call(spread_kernel, out_shape=(jax.ShapeDtypeStruct((slots_tota...  7.13 us
    dot_general x1, matrix products, body(): before = jnp.dot(earlier, owner_hot, preferred_element_type=jnp.float32)  2.27 us

profile of v2, /device:TPU:11, one launch (start us, length us, event | category | flops | bytes accessed | tf_op | source)
XLA Modules:
  0.0 81.8 jit_solution(11821226231334083184)
XLA Ops:
  0.6 0.0 copy-start
  0.6 0.0 copy-start.1
  0.7 0.0 copy-start.2
  0.7 2.3 %fusion.2 = f32[2048]{0:T(1024)S(1)} fusion(s32[2048]{0:T(1024)} %bitcast.8), kind=kOutput, calls=%fused_computation.3 | convolution fusion | flops 273020928 | bytes 16384 | tf_op jit(solution)/shard_map/dot_general | solution.py:251
  2.9 0.0 copy-done
  3.0 0.0 copy-done.1
  3.0 0.0 copy-done.2
  3.0 0.6 add_select_fusion
  3.6 0.9 %convolution_convert_fusion.counts_ref = s32[10,128]{1,0:T(8,128)} fusion(s32[2048]{0:T(1024)S(1)} %copy-done.2, s32[2048]{0:T(1024)S(1)} %get-tuple-element.12), kind=kOutput, calls=%fused_computation.4 | convolution fusion | flops 5526784 | bytes 21504 | tf_op jit(solution)/shard_map/dot_general | solution.py:282
  4.5 0.6 broadcast_in_dim.2.fill_ref
  5.1 7.1 %spread.1 = (f32[4096,128]{1,0:T(8,128)}, s32[4096]{0:T(1024)}) custom-call(s32[2048]{0:T(1024)} %get-tuple-element.13.target_ref, s32[2048]{0:T(1024)} %get-tuple-element.14.key_ref, s32[4096]{0:T(1024)} %broadcast_in_dim.2.fill_ref, f32[2048,128]{1,0:T(8,128)} %values_ref.1), custom_call_target="tpu_custom_call" | custom-call | tf_op jit(solution)/shard_map/spread/pallas_call | solution.py:260
  12.2 54.8 %exchange.1 = (f32[32,128,128]{2,1,0:T(8,128)}, s32[32,1,128]{2,1,0:T(1,128)}, s32[10,128]{1,0:T(8,128)}) custom-call(f32[32,128,128]{2,1,0:T(8,128)} %bitcast.5, s32[32,1,128]{2,1,0:T(1,128)} %bitcast.7, s32[10,128]{1,0:T(8,128)} %convolution_convert_fusion.counts_ref), custom_call_target="tpu_custom_call" | custom-call | tf_op jit(solution)/shard_map/exchange/pallas_call | solution.py:287
  67.0 0.0 copy-start.3
  67.0 14.2 %place.1 = f32[40,13824]{1,0:T(8,128)} custom-call(s32[32,1,128]{2,1,0:T(1,128)} %get-tuple-element.9.keys_ref, f32[4096,128]{1,0:T(8,128)} %bitcast.6), custom_call_target="tpu_custom_call" | custom-call | tf_op jit(solution)/shard_map/place/pallas_call | solution.py:319
  81.2 0.0 copy-done.3
  81.2 0.6 copy.7
Async XLA Ops:
  0.6 2.3 %copy-start = (s32[2048]{0:T(1024)S(1)}, s32[2048]{0:T(1024)}, u32[]{:S(2)}) copy-start(s32[2048]{0:T(1024)} %param.6) | copy-start | bytes 24580
  0.6 2.3 %copy-start.1 = (s32[2048,1]{0,1:T(1,128)S(1)}, s32[2048,1]{0,1:T(1,128)}, u32[]{:S(2)}) copy-start(s32[2048,1]{0,1:T(1,128)} %param.5) | copy-start | bytes 24580
  0.7 2.3 %copy-start.2 = (s32[2048]{0:T(1024)S(1)}, s32[2048]{0:T(1024)}, u32[]{:S(2)}) copy-start(s32[2048]{0:T(1024)} %param.7) | copy-start | bytes 24580
  67.0 14.2 %copy-start.3 = (s32[10,128]{1,0:T(8,128)S(1)}, s32[10,128]{1,0:T(8,128)}, u32[]{:S(2)}) copy-start(s32[10,128]{1,0:T(8,128)} %get-tuple-element.11) | copy-start | bytes 15364

commit v3 on v2

--- a/solution.py
+++ b/solution.py
@@ -13,7 +13,7 @@
 ROWS_DEV = 40
 SUB = 8
 MESH = pl.DeviceIdType.MESH
-CHAINS = 4
+CHAINS = 8
 
 
 def spread_kernel(target_ref, key_ref, fill_ref, values_ref, send_ref, keys_ref, sem):
@@ -63,16 +63,18 @@
     barrier = pltpu.get_barrier_semaphore()
 
     paired = rows & (rows - 1) == 0
-    order = [rows // 2] + [d for d in range(1, rows) if d != rows // 2] + [0]
+    half = rows // 2
+    near, far = list(range(1, half)), list(range(half, rows))
+    inside = far + near + [0]
+    outside = near + [0] + far if paired else inside
+    beside = ((r + 1) // half) * ((rows - r) // half) if rows > 2 else 1
 
     def partner(at, d):
         if not paired:
             return lax.rem(at + d, rows)
-        out, bit = at, 1
+        out, bit = 0, 1
         while bit < rows:
-            if d & bit:
-                half = lax.rem(out // bit, 2)
-                out = out + bit - 2 * bit * half
+            out = out + bit * lax.rem(at // bit + d // bit, 2)
             bit *= 2
         return out
 
@@ -132,14 +134,15 @@
         plane_copy(k).start()
 
     def for_all(act):
-        for d in order:
+        for out, ins in zip(outside, inside):
+            d = out + beside * (ins - out)
 
             def one(e, carry):
                 for copy in value_copies(d, e):
                     act(copy)
                 return carry
 
-            lax.fori_loop(0 if d else 1, cols, one, 0)
+            lax.fori_loop(1 - (d + rows - 1) // rows, cols, one, 0)
 
     for_all(lambda copy: copy.start())
     own_in = pltpu.make_async_copy(send_ref.at[me], own, local_sem.at[0])
@@ -190,7 +193,6 @@
     sources, _, capacity = keys_ref.shape
     cells = accs[0].shape[0] - SUB
     tiles = cells // ROWS_DEV
-    unit = math.gcd(capacity, 32)
 
     @pl.when(step == 0)
     def _():
@@ -198,20 +200,16 @@
             acc[...] = jnp.zeros_like(acc)
 
     def source(s, carry):
-        def group(g, carry):
-            base = pl.multiple_of(g * unit, unit)
-            row = pl.multiple_of(s * capacity + base, unit)
-            at = [keys_ref[s, 0, base + j] for j in range(unit)]
-            for j in range(0, unit, CHAINS):
-                sums = [
-                    accs[q][pl.ds(at[j + q], 1), :] + values_ref[pl.ds(row + j + q, 1), :]
-                    for q in range(CHAINS)
-                ]
-                for q in range(CHAINS):
-                    accs[q][pl.ds(at[j + q], 1), :] = sums[q]
-            return carry
-
-        return lax.fori_loop(0, capacity // unit, group, carry)
+        row = pl.multiple_of(s * capacity, capacity)
+        for j in range(0, capacity, CHAINS):
+            at = [keys_ref[s, 0, j + q] for q in range(CHAINS)]
+            sums = [
+                accs[q][pl.ds(at[q], 1), :] + values_ref[pl.ds(row + j + q, 1), :]
+                for q in range(CHAINS)
+            ]
+            for q in range(CHAINS):
+                accs[q][pl.ds(at[q], 1), :] = sums[q]
+        return carry
 
     lax.fori_loop(0, sources, source, 0)
 

time: 82.2 us -> 77.1 us (0.938)
  Pallas kernels: 76.1 us -> 70.9 us
    pallas_call x1, Pallas kernels: 14.2 us -> 8.89 us  [body(): pl.pallas_call(place_kernel, out_shape=jax.ShapeDtypeStruct((ROWS_DEV, F)...]
where the time goes in v3:
time: 77.1 us; the launch traced here: 76.7 us
  Pallas kernels  70.9 us (92%)
  matrix products  3.15 us (4%)
  local copies, waits for them, and re-layouts  1.22 us (2%)
    pallas_call x1, Pallas kernels, body(): pl.pallas_call(functools.partial(exchange_kernel, size_row, size_col), ou...  54.9 us
    pallas_call x1, Pallas kernels, body(): pl.pallas_call(place_kernel, out_shape=jax.ShapeDtypeStruct((ROWS_DEV, F)...  8.89 us
    pallas_call x1, Pallas kernels, body(): pl.pallas_call(spread_kernel, out_shape=(jax.ShapeDtypeStruct((slots_tota...  7.13 us
    dot_general x1, matrix products, body(): before = jnp.dot(earlier, owner_hot, preferred_element_type=jnp.float32)  2.27 us

profile of v3, /device:TPU:11, one launch (start us, length us, event | category | flops | bytes accessed | tf_op | source)
XLA Modules:
  0.0 76.7 jit_solution(2891027900091879258)
XLA Ops:
  0.6 0.0 copy-start
  0.6 0.0 copy-start.1
  0.7 0.0 copy-start.2
  0.7 2.3 %fusion.2 = f32[2048]{0:T(1024)S(1)} fusion(s32[2048]{0:T(1024)} %bitcast.8), kind=kOutput, calls=%fused_computation.3 | convolution fusion | flops 273020928 | bytes 16384 | tf_op jit(solution)/shard_map/dot_general | solution.py:249
  2.9 0.0 copy-done
  3.0 0.0 copy-done.1
  3.0 0.0 copy-done.2
  3.0 0.6 add_select_fusion
  3.6 0.9 %convolution_convert_fusion.counts_ref = s32[10,128]{1,0:T(8,128)} fusion(s32[2048]{0:T(1024)S(1)} %copy-done.2, s32[2048]{0:T(1024)S(1)} %get-tuple-element.12), kind=kOutput, calls=%fused_computation.4 | convolution fusion | flops 5526784 | bytes 21504 | tf_op jit(solution)/shard_map/dot_general | solution.py:280
  4.5 0.6 broadcast_in_dim.2.fill_ref
  5.1 7.1 %spread.1 = (f32[4096,128]{1,0:T(8,128)}, s32[4096]{0:T(1024)}) custom-call(s32[2048]{0:T(1024)} %get-tuple-element.13.target_ref, s32[2048]{0:T(1024)} %get-tuple-element.14.key_ref, s32[4096]{0:T(1024)} %broadcast_in_dim.2.fill_ref, f32[2048,128]{1,0:T(8,128)} %values_ref.1), custom_call_target="tpu_custom_call" | custom-call | tf_op jit(solution)/shard_map/spread/pallas_call | solution.py:258
  12.2 54.9 %exchange.1 = (f32[32,128,128]{2,1,0:T(8,128)}, s32[32,1,128]{2,1,0:T(1,128)}, s32[10,128]{1,0:T(8,128)}) custom-call(f32[32,128,128]{2,1,0:T(8,128)} %bitcast.5, s32[32,1,128]{2,1,0:T(1,128)} %bitcast.7, s32[10,128]{1,0:T(8,128)} %convolution_convert_fusion.counts_ref), custom_call_target="tpu_custom_call" | custom-call | tf_op jit(solution)/shard_map/exchange/pallas_call | solution.py:285
  67.1 0.0 copy-start.3
  67.2 8.9 %place.1 = f32[40,13824]{1,0:T(8,128)} custom-call(s32[32,1,128]{2,1,0:T(1,128)} %get-tuple-element.9.keys_ref, f32[4096,128]{1,0:T(8,128)} %bitcast.6), custom_call_target="tpu_custom_call" | custom-call | tf_op jit(solution)/shard_map/place/pallas_call | solution.py:317
  76.0 0.0 copy-done.3
  76.1 0.6 copy.7
Async XLA Ops:
  0.6 2.3 %copy-start = (s32[2048]{0:T(1024)S(1)}, s32[2048]{0:T(1024)}, u32[]{:S(2)}) copy-start(s32[2048]{0:T(1024)} %param.6) | copy-start | bytes 24580
  0.6 2.3 %copy-start.1 = (s32[2048,1]{0,1:T(1,128)S(1)}, s32[2048,1]{0,1:T(1,128)}, u32[]{:S(2)}) copy-start(s32[2048,1]{0,1:T(1,128)} %param.5) | copy-start | bytes 24580
  0.7 2.3 %copy-start.2 = (s32[2048]{0:T(1024)S(1)}, s32[2048]{0:T(1024)}, u32[]{:S(2)}) copy-start(s32[2048]{0:T(1024)} %param.7) | copy-start | bytes 24580
  67.1 8.9 %copy-start.3 = (s32[10,128]{1,0:T(8,128)S(1)}, s32[10,128]{1,0:T(8,128)}, u32[]{:S(2)}) copy-start(s32[10,128]{1,0:T(8,128)} %get-tuple-element.11) | copy-start | bytes 15364

commit v4 on v3

--- a/solution.py
+++ b/solution.py
@@ -20,16 +20,18 @@
     fill = pltpu.make_async_copy(fill_ref, keys_ref, sem)
     fill.start()
     fill.wait()
-    step = math.gcd(values_ref.shape[0], 16)
+    step, part = math.gcd(values_ref.shape[0], 128), math.gcd(values_ref.shape[0], 16)
 
     def group(g, carry):
         base = pl.multiple_of(g * step, step)
-        to = [target_ref[base + i] for i in range(step)]
-        keys = [key_ref[base + i] for i in range(step)]
-        for i in range(step):
-            send_ref[pl.ds(to[i], 1), :] = values_ref[pl.ds(base + i, 1), :]
-        for i in range(step):
-            keys_ref[to[i]] = keys[i]
+        for j in range(0, step, part):
+            spots = range(j, j + part)
+            to = [target_ref[base + i] for i in spots]
+            keys = [key_ref[base + i] for i in spots]
+            for i in spots:
+                send_ref[pl.ds(to[i - j], 1), :] = values_ref[pl.ds(base + i, 1), :]
+            for i in spots:
+                keys_ref[to[i - j]] = keys[i - j]
         return carry
 
     lax.fori_loop(0, values_ref.shape[0] // step, group, 0)
@@ -187,7 +189,7 @@
     lax.fori_loop(1, cols, add_every, 0)
 
 
-def place_kernel(keys_ref, values_ref, out_ref, *rest):
+def place_kernel(keys_ref, values_ref, total_ref, out_ref, occupancy_ref, *rest):
     accs, (outbuf, sems) = rest[:CHAINS], rest[CHAINS:]
     step = pl.program_id(0)
     sources, _, capacity = keys_ref.shape
@@ -196,6 +198,7 @@
 
     @pl.when(step == 0)
     def _():
+        occupancy_ref[...] = total_ref[:, :tiles]
         for acc in accs:
             acc[...] = jnp.zeros_like(acc)
 
@@ -314,20 +317,24 @@
     )
 
     batch = math.gcd(devices_all, 4)
-    summed = pl.pallas_call(
+    summed, occupancy = pl.pallas_call(
         place_kernel,
-        out_shape=jax.ShapeDtypeStruct((ROWS_DEV, F), jnp.float32),
+        out_shape=(
+            jax.ShapeDtypeStruct((ROWS_DEV, F), jnp.float32),
+            jax.ShapeDtypeStruct((tile_rows, tiles_count), jnp.int32),
+        ),
         grid=(devices_all // batch,),
         in_specs=[
             pl.BlockSpec((batch, 1, capacity), lambda i: (i, 0, 0), memory_space=pltpu.SMEM),
             pl.BlockSpec((batch * capacity, TILE), lambda i: (i, 0)),
+            vmem,
         ],
-        out_specs=anywhere,
+        out_specs=(anywhere, vmem),
         scratch_shapes=[pltpu.VMEM((cells + SUB, TILE), jnp.float32)] * CHAINS
         + [pltpu.VMEM((ROWS_DEV, F), jnp.float32), sems((ROWS_DEV // SUB,))],
         name="place",
-    )(got_keys, got.reshape(slots_total, TILE))
-    return (summed, total[:, :tiles_count])
+    )(got_keys, got.reshape(slots_total, TILE), total)
+    return (summed, occupancy)
 
 
 def solution(mesh):

time: 77.1 us -> 76.9 us (level)
  no operation moved by 1% of the time
where the time goes in v4:
time: 76.9 us; the launch traced here: 76.4 us
  Pallas kernels  71.3 us (93%)
  matrix products  3.16 us (4%)
    pallas_call x1, Pallas kernels, body(): pl.pallas_call(functools.partial(exchange_kernel, size_row, size_col), ou...  54.9 us
    pallas_call x1, Pallas kernels, body(): pl.pallas_call(place_kernel, out_shape=(jax.ShapeDtypeStruct((ROWS_DEV, F...  9.48 us
    pallas_call x1, Pallas kernels, body(): pl.pallas_call(spread_kernel, out_shape=(jax.ShapeDtypeStruct((slots_tota...  6.92 us
    dot_general x1, matrix products, body(): before = jnp.dot(earlier, owner_hot, preferred_element_type=jnp.float32)  2.27 us

profile of v4, /device:TPU:11, one launch (start us, length us, event | category | flops | bytes accessed | tf_op | source)
XLA Modules:
  0.0 76.4 jit_solution(16667820938503063754)
XLA Ops:
  0.6 0.0 copy-start
  0.6 0.0 copy-start.1
  0.7 0.0 copy-start.2
  0.7 2.3 %fusion.2 = f32[2048]{0:T(1024)S(1)} fusion(s32[2048]{0:T(1024)} %bitcast.7), kind=kOutput, calls=%fused_computation.3 | convolution fusion | flops 273020928 | bytes 16384 | tf_op jit(solution)/shard_map/dot_general | solution.py:252
  2.9 0.0 copy-done
  3.0 0.0 copy-done.1
  3.0 0.0 copy-done.2
  3.0 0.6 add_select_fusion
  3.6 0.9 %convolution_convert_fusion.counts_ref = s32[10,128]{1,0:T(8,128)} fusion(s32[2048]{0:T(1024)S(1)} %copy-done.2, s32[2048]{0:T(1024)S(1)} %get-tuple-element.12), kind=kOutput, calls=%fused_computation.4 | convolution fusion | flops 5526784 | bytes 21504 | tf_op jit(solution)/shard_map/dot_general | solution.py:283
  4.5 0.6 broadcast_in_dim.2.fill_ref
  5.1 6.9 %spread.1 = (f32[4096,128]{1,0:T(8,128)}, s32[4096]{0:T(1024)}) custom-call(s32[2048]{0:T(1024)} %get-tuple-element.13.target_ref, s32[2048]{0:T(1024)} %get-tuple-element.14.key_ref, s32[4096]{0:T(1024)} %broadcast_in_dim.2.fill_ref, f32[2048,128]{1,0:T(8,128)} %values_ref.1), custom_call_target="tpu_custom_call" | custom-call | tf_op jit(solution)/shard_map/spread/pallas_call | solution.py:261
  12.0 54.9 %exchange.1 = (f32[32,128,128]{2,1,0:T(8,128)}, s32[32,1,128]{2,1,0:T(1,128)}, s32[10,128]{1,0:T(8,128)}) custom-call(f32[32,128,128]{2,1,0:T(8,128)} %bitcast.4, s32[32,1,128]{2,1,0:T(1,128)} %bitcast.6, s32[10,128]{1,0:T(8,128)} %convolution_convert_fusion.counts_ref), custom_call_target="tpu_custom_call" | custom-call | tf_op jit(solution)/shard_map/exchange/pallas_call | solution.py:288
  66.9 9.5 %place.1 = (f32[40,13824]{1,0:T(8,128)}, s32[10,108]{1,0:T(8,128)}) custom-call(s32[32,1,128]{2,1,0:T(1,128)} %get-tuple-element.9.keys_ref, f32[4096,128]{1,0:T(8,128)} %bitcast.5, s32[10,128]{1,0:T(8,128)} %get-tuple-element.11.total_ref), custom_call_target="tpu_custom_call" | custom-call | tf_op jit(solution)/shard_map/place/pallas_call | solution.py:320
Async XLA Ops:
  0.6 2.3 %copy-start = (s32[2048]{0:T(1024)S(1)}, s32[2048]{0:T(1024)}, u32[]{:S(2)}) copy-start(s32[2048]{0:T(1024)} %param.6) | copy-start | bytes 24580
  0.6 2.3 %copy-start.1 = (s32[2048,1]{0,1:T(1,128)S(1)}, s32[2048,1]{0,1:T(1,128)}, u32[]{:S(2)}) copy-start(s32[2048,1]{0,1:T(1,128)} %param.5) | copy-start | bytes 24580
  0.7 2.3 %copy-start.2 = (s32[2048]{0:T(1024)S(1)}, s32[2048]{0:T(1024)}, u32[]{:S(2)}) copy-start(s32[2048]{0:T(1024)} %param.7) | copy-start | bytes 24580
